TPU v7x, 32 devices: a whole 2x2x4 slice. The times are simulated.
32 devices in a mesh: groups: 2 (over y), seq: 4 (over z), tensor: 4 (over x, core).
Axes of the slice: x: 2, y: 2, z: 4, core: 2. Of those that a mesh axis runs over, the one named last changes fastest.
Arguments:
- final_block_queries: bfloat16 [256, 8192], P(('groups', 'seq'), 'tensor'), parts along dimension 0, may hold values from -96 to 96
- final_block_keys: bfloat16 [256, 1024], P(('groups', 'seq'), 'tensor'), parts along dimension 0, may hold values from -16 to 16
- final_block_values: bfloat16 [256, 1024], P(('groups', 'seq'), 'tensor'), parts along dimension 0, may hold values from -6 to 6
- prompt_cached_keys: bfloat16 [12288, 1024], P(('groups', 'seq'), 'tensor'), parts along dimension 0, may hold values from -16 to 16
- prompt_cached_values: bfloat16 [12288, 1024], P(('groups', 'seq'), 'tensor'), parts along dimension 0, may hold values from -6 to 6
- paged_cache_pool: bfloat16 [256, 128, 2, 1024], P(('groups', 'seq'), None, None, 'tensor'), parts along dimension 0, may hold values from -16 to 16
- step_slot_queries: bfloat16 [32, 4, 8192], P(('groups', 'seq'), None, 'tensor'), parts along dimension 0, may hold values from -96 to 96
- step_token_keys: bfloat16 [32, 4, 1024], P(('groups', 'seq'), None, 'tensor'), parts along dimension 0, may hold values from -16 to 16
- step_token_values: bfloat16 [32, 4, 1024], P(('groups', 'seq'), None, 'tensor'), parts along dimension 0, may hold values from -6 to 6
- normed_step_inputs: bfloat16 [32, 4, 8192], P(('groups', 'seq'), None, 'tensor'), parts along dimension 0, may hold values from -6 to 6
- adapter_down_maps: bfloat16 [8192, 128], P('tensor'), may hold values from -0.0625 to 0.0625
- adapter_up_maps: bfloat16 [128, 8192], P(None, 'tensor'), may hold values from -1.5 to 1.5
- slot_request: int32 [32], P('groups'), parts along dimension 0, may hold values from 0 to 15, as said below
- request_page_table: int32 [32, 8], P('groups'), parts along dimension 0, may hold values from 0 to 127, as said below
- lengths: int32 [32], P('groups'), parts along dimension 0, may hold values from 2 to 1024, as said below
- request_adapter: int32 [32], P('groups'), parts along dimension 0, may hold values from 0 to 7
- request_rank: int32 [32], P('groups'), parts along dimension 0, may hold values from 4 to 16
Outputs:
- prefill_out: bfloat16 [256, 8192], P(('groups', 'seq'), 'tensor'), parts along dimension 0
- decode_out: bfloat16 [32, 4, 8192], P(('groups', 'seq'), None, 'tensor'), parts along dimension 0
There are 2 independent parts, one for each index of `groups`. A program takes and returns all parts, laid end to end along the dimension named above; an argument that names none is the same for every part. Nothing has to cross between parts.
Inputs may be any that keep to these rules, and one draw needn't show every extreme that they name: A permutation: slot k serves request slot_request[k]; the owner of slots k * 4 to (k + 1) * 4 - 1 is owner k. `request_page_table`: every pool page is named exactly once. For every owner and every block of 32 pool pages (pages b * 32 to (b + 1) * 32 - 1), exactly 8 of the pages of that owner's requests lie in the block. `lengths`: some request has exactly 1024 cached tokens.
All inputs are finite; a program needn't handle non-finite values.
Results may differ from a plain program's by a relative error of at most 0.028.
Values may be sent and summed in bfloat16 or wider, within the bound.
No kernel may reach another device: no remote copies, remote signals or barrier semaphores. Data moves between devices by JAX's collectives and lax.ppermute only.
A program may use at most 128 MiB of HBM per device.

v0:
```python
import jax
import jax.numpy as jnp
from jax import lax
from jax.sharding import PartitionSpec as P

HEAD_SIZE = 128
LARGEST_RANK = 16
MASKED = -1e30


def lookup_rows(lookup, positions):
    hit_mask = positions[..., None] == jnp.arange(lookup.shape[0], dtype=jnp.int32)
    if lookup.ndim == 1:
        return jnp.sum(jnp.where(hit_mask, lookup, 0), axis=-1)
    return jnp.sum(jnp.where(hit_mask[..., None], lookup, 0), axis=-2)


def partial_softmax(query_vectors, paged_key_rows, paged_value_rows, allowed):
    batch_count, query_total_count, query_width = query_vectors.shape
    kv_heads = paged_key_rows.shape[2] // HEAD_SIZE
    heads_per_group = query_width // HEAD_SIZE // kv_heads
    query_head_rows = query_vectors.reshape(
        batch_count, query_total_count, kv_heads, heads_per_group, HEAD_SIZE
    )
    key_head_rows = paged_key_rows.reshape(
        batch_count, paged_key_rows.shape[1], kv_heads, HEAD_SIZE
    )
    value_head_rows = paged_value_rows.reshape(
        batch_count, paged_value_rows.shape[1], kv_heads, HEAD_SIZE
    )
    scores = jnp.einsum(
        "etkgd,epkd->ekgtp", query_head_rows, key_head_rows, preferred_element_type=jnp.float32
    ) * HEAD_SIZE ** (-0.5)
    key_mask = allowed[:, None, None, :, :]
    scores = jnp.where(key_mask, scores, MASKED)
    row_max = jnp.max(scores, axis=-1)
    weights = jnp.where(key_mask, jnp.exp(scores - row_max[..., None]), 0.0)
    row_total = jnp.sum(weights, axis=-1)
    summed = jnp.einsum(
        "ekgtp,epkd->etkgd",
        weights.astype(jnp.bfloat16),
        value_head_rows,
        preferred_element_type=jnp.float32,
    )
    heads_here = kv_heads * heads_per_group
    row_max = jnp.transpose(row_max, (0, 3, 1, 2)).reshape(
        batch_count, query_total_count, heads_here
    )
    row_total = jnp.transpose(row_total, (0, 3, 1, 2)).reshape(
        batch_count, query_total_count, heads_here
    )
    return (
        summed.reshape(batch_count, query_total_count, heads_here, HEAD_SIZE),
        row_max,
        row_total,
    )


def combine(summed, row_max, row_total, along):
    best_max = jnp.max(row_max, axis=along, keepdims=True)
    factor = jnp.exp(row_max - best_max)
    whole_total = jnp.sum(factor * row_total, axis=along)
    merged = jnp.sum(factor[..., None] * summed, axis=along)
    return merged / whole_total[..., None]


def per_device(
    final_block_queries,
    final_block_keys,
    final_block_values,
    prompt_cached_keys,
    prompt_cached_values,
    paged_cache_pool,
    step_slot_queries,
    step_token_keys,
    step_token_values,
    normed_step_inputs,
    adapter_down_maps,
    adapter_up_maps,
    slot_request,
    request_page_table,
    lengths,
    request_adapter,
    request_rank,
):
    seq_count = lax.axis_size("seq")
    position = lax.axis_index("seq")
    span_rows = final_block_queries.shape[0]
    ctx_rows = prompt_cached_keys.shape[0]
    heads_here = final_block_queries.shape[1] // HEAD_SIZE
    everyone = lax.all_gather(final_block_queries, "seq", axis=0, tiled=True)
    span_total = everyone.shape[0]
    block_rows = min(128, span_total)
    paged_key_rows = jnp.concatenate([prompt_cached_keys, final_block_keys], axis=0)
    paged_value_rows = jnp.concatenate([prompt_cached_values, final_block_values], axis=0)
    spots = jnp.arange(paged_key_rows.shape[0], dtype=jnp.int32)
    key_pos = jnp.where(spots < ctx_rows, -1, position * span_rows + spots - ctx_rows)

    def run_block(row_start):
        query_rows = lax.dynamic_slice_in_dim(everyone, row_start, block_rows, 0)
        row_pos = row_start + jnp.arange(block_rows, dtype=jnp.int32)
        allowed = key_pos[None, :] <= row_pos[:, None]
        summed, row_max, row_total = partial_softmax(
            query_rows[None], paged_key_rows[None], paged_value_rows[None], allowed[None]
        )
        return (summed[0], row_max[0], row_total[0])

    starts = jnp.arange(span_total // block_rows, dtype=jnp.int32) * block_rows
    summed, row_max, row_total = lax.map(run_block, starts)
    summed = summed.reshape(span_total, heads_here, HEAD_SIZE)
    row_max = row_max.reshape(span_total, heads_here)
    row_total = row_total.reshape(span_total, heads_here)
    returned = (
        lax.all_to_all(summed, "seq", split_axis=0, concat_axis=0, tiled=True),
        lax.all_to_all(row_max, "seq", split_axis=0, concat_axis=0, tiled=True),
        lax.all_to_all(row_total, "seq", split_axis=0, concat_axis=0, tiled=True),
    )
    block_sums = returned[0].reshape(seq_count, span_rows, heads_here, HEAD_SIZE)
    block_maxes = returned[1].reshape(seq_count, span_rows, heads_here)
    block_totals = returned[2].reshape(seq_count, span_rows, heads_here)
    prefill_out = (
        combine(block_sums, block_maxes, block_totals, 0)
        .reshape(span_rows, heads_here * HEAD_SIZE)
        .astype(jnp.bfloat16)
    )
    slots_total = slot_request.shape[0]
    slots_here = slots_total // seq_count
    page_count = request_page_table.shape[1]
    pool_here = paged_cache_pool.shape[0]
    page_len = paged_cache_pool.shape[1]
    per_owner = slots_here * page_count // seq_count
    entries = slots_here * page_count
    decode_step_count = step_slot_queries.shape[1]
    slot_page_list = lookup_rows(request_page_table, slot_request)
    slot_length = lookup_rows(lengths, slot_request)
    owner_pages = slot_page_list.reshape(seq_count, entries)
    holder = owner_pages // pool_here
    pool_place = owner_pages % pool_here
    is_mine = holder == position
    rank_in = jnp.cumsum(is_mine.astype(jnp.int32), axis=1) - 1
    hit_mask = is_mine[:, :, None] & (rank_in[:, :, None] == jnp.arange(per_owner, dtype=jnp.int32))
    send_place = jnp.sum(jnp.where(hit_mask, pool_place[:, :, None], 0), axis=1).reshape(-1)
    entry_ids = jnp.arange(entries, dtype=jnp.int32)
    outgoing = paged_cache_pool[send_place]
    my_holder = lax.dynamic_index_in_dim(holder, position, 0, keepdims=False)
    before = (my_holder[None, :] == my_holder[:, None]) & (entry_ids[None, :] < entry_ids[:, None])
    arrive = my_holder * per_owner + jnp.sum(before.astype(jnp.int32), axis=1)
    my_requests = lax.dynamic_slice_in_dim(slot_request, position * slots_here, slots_here)
    my_lengths = lax.dynamic_slice_in_dim(slot_length, position * slots_here, slots_here)
    adapters = lookup_rows(request_adapter, my_requests)
    ranks = lookup_rows(request_rank, my_requests)
    hidden_input_rows = normed_step_inputs.reshape(
        slots_here * decode_step_count, normed_step_inputs.shape[2]
    )
    reduced_rank_state = lax.psum(
        jnp.dot(hidden_input_rows, adapter_down_maps, preferred_element_type=jnp.float32), "tensor"
    )
    column_indices = jnp.arange(adapter_down_maps.shape[1], dtype=jnp.int32)
    rank_keep_mask = (column_indices[None, :] // LARGEST_RANK == adapters[:, None]) & (
        column_indices[None, :] % LARGEST_RANK < ranks[:, None]
    )
    adapter_kept_rank = jnp.where(
        jnp.repeat(rank_keep_mask, decode_step_count, axis=0), reduced_rank_state, 0.0
    ).astype(jnp.bfloat16)
    raised_queries = jnp.dot(
        adapter_kept_rank, adapter_up_maps, preferred_element_type=jnp.float32
    ).reshape(slots_here, decode_step_count, -1)
    query_vectors = (step_slot_queries.astype(jnp.float32) + raised_queries).astype(jnp.bfloat16)
    step_pos = jnp.arange(decode_step_count, dtype=jnp.int32)
    fresh_ok = step_pos[None, :] <= step_pos[:, None]
    incoming = lax.all_to_all(outgoing, "seq", split_axis=0, concat_axis=0, tiled=True)
    gathered_pages = incoming[arrive].reshape(slots_here, page_count * page_len, 2, -1)
    all_keys = jnp.concatenate([gathered_pages[:, :, 0], step_token_keys], axis=1)
    all_values = jnp.concatenate([gathered_pages[:, :, 1], step_token_values], axis=1)
    cache_pos = jnp.arange(page_count * page_len, dtype=jnp.int32)
    cache_ok = jnp.broadcast_to(
        cache_pos[None, None, :] < my_lengths[:, None, None],
        (slots_here, decode_step_count, page_count * page_len),
    )
    allowed = jnp.concatenate(
        [
            cache_ok,
            jnp.broadcast_to(fresh_ok[None], (slots_here, decode_step_count, decode_step_count)),
        ],
        axis=2,
    )
    summed, row_max, row_total = partial_softmax(query_vectors, all_keys, all_values, allowed)
    decode_out = (
        (summed / row_total[..., None])
        .reshape(slots_here, decode_step_count, -1)
        .astype(jnp.bfloat16)
    )
    return (prefill_out, decode_out)


def solution(mesh):
    placed = (
        P(("groups", "seq"), "tensor"),
        P(("groups", "seq"), "tensor"),
        P(("groups", "seq"), "tensor"),
        P(("groups", "seq"), "tensor"),
        P(("groups", "seq"), "tensor"),
        P(("groups", "seq"), None, None, "tensor"),
        P(("groups", "seq"), None, "tensor"),
        P(("groups", "seq"), None, "tensor"),
        P(("groups", "seq"), None, "tensor"),
        P(("groups", "seq"), None, "tensor"),
        P("tensor", None),
        P(None, "tensor"),
        P("groups"),
        P("groups", None),
        P("groups"),
        P("groups"),
        P("groups"),
    )
    return jax.shard_map(
        per_device,
        mesh=mesh,
        in_specs=placed,
        out_specs=(P(("groups", "seq"), "tensor"), P(("groups", "seq"), None, "tensor")),
        check_vma=False,
    )
```

profile of v0, /device:TPU:0, one launch (start us, length us, event | category | flops | bytes accessed | tf_op | source)
XLA Modules:
  0.0 200.9 jit_solution(16508769630650685992)
XLA Ops:
  0.9 1.2 pad_maximum_fusion
  2.2 0.7 copy.124
  2.8 17.6 %all_gather.3 = bf16[128,2048]{1,0:T(8,128)(2,1)S(1)} all-gather(bf16[32,2048]{1,0:T(8,128)(2,1)} %param.17), channel_id=1, replica_groups=mesh['groups'=2,'seq'=4,'tensor'=4] {'seq'}, dimensions={0}, use_global_device_ids=true | all-gather | bytes 655360 | tf_op jit(solution)/shard_map/all_gather | solution.py:91
  20.7 2.0 %fusion.1 = (f32[2,8,128]{2,1,0:T(8,128)S(1)}, f32[2,1568,128,8]{2,1,3,0:T(8,128)S(1)}) fusion(pred[128,1568]{0,1:T(8,128)(4,1)S(1)} %iota_compare_fusion, bf16[1568,2,128,1]{0,2,3,1:T(8,128)(2,1)S(1)} %bitcast.128, bf16[128,2,8,128]{0,3,2,1:T(8,128)(2,1)S(1)} %bitcast.129), kind=kOutput, calls=%fused_computation.5 | convolution fusion | flops 831715328 | bytes 14381056 | tf_op jit(solution)/shard_map/while/body/eval_jaxpr/etkgd,epkd->ekgtp/dot_general | solution.py:31
  22.8 3.0 %fusion.2 = f32[2,8,128]{2,1,0:T(8,128)S(1)} fusion(f32[2,1568,128,8]{2,1,3,0:T(8,128)S(1)} %get-tuple-element.36, f32[2,8,128]{2,1,0:T(8,128)S(1)} %get-tuple-element.35, pred[128,1568]{0,1:T(8,128)(4,1)S(1)} %iota_compare_fusion), kind=kLoop, calls=%fused_computation.6 | loop fusion | flops 16054272 | bytes 13062144 | tf_op jit(solution)/shard_map/while/body/eval_jaxpr/reduce_sum | solution.py:38
  25.8 1.5 copy-done.1
  27.4 0.7 reshape.433
  28.1 5.4 %all-to-all-start.2 = ((f32[4,1,512]{2,1,0:T(1,128)}), f32[4,1,512]{2,1,0:T(1,128)S(1)}, u32[]{:S(2)}, u32[]{:S(2)}) async-start(f32[4,1,512]{2,1,0:T(1,128)} %reshape.433), calls=%async_computation.2 | async-start | bytes 16384 | tf_op jit(solution)/shard_map/all_to_all | solution.py:116
  33.7 0.7 reshape.431
  35.0 4.1 %all-to-all-done.2 = f32[4,1,512]{2,1,0:T(1,128)S(1)} async-done(((f32[4,1,512]{2,1,0:T(1,128)}), f32[4,1,512]{2,1,0:T(1,128)S(1)}, u32[]{:S(2)}, u32[]{:S(2)}) %all-to-all-start.2) | async-done | bytes 8224 | tf_op jit(solution)/shard_map/all_to_all | solution.py:116
  39.1 3.2 %all-to-all-start = ((f32[4,1,512]{2,1,0:T(1,128)}), f32[4,1,512]{2,1,0:T(1,128)S(1)}, u32[]{:S(2)}, u32[]{:S(2)}) async-start(f32[4,1,512]{2,1,0:T(1,128)} %reshape.431), calls=%async_computation | async-start | bytes 16384 | tf_op jit(solution)/shard_map/all_to_all | solution.py:115
  42.4 6.5 %fusion.5 = f32[2,128,8,128]{3,1,2,0:T(8,128)S(1)} fusion(bf16[1568,2,128,1]{0,2,3,1:T(8,128)(2,1)S(1)} %bitcast.131, f32[2,1568,128,8]{2,1,3,0:T(8,128)} %copy-done.1, f32[2,8,128]{2,1,0:T(8,128)S(1)} %get-tuple-element.35, pred[128,1568]{0,1:T(8,128)(4,1)S(1)} %iota_compare_fusion), kind=kOutput, calls=%fused_computation.9 | convolution fusion | flops 838139904 | bytes 14905344 | tf_op jit(solution)/shard_map/while/body/eval_jaxpr/ekgtp,epkd->etkgd/dot_general | solution.py:39
  48.9 1.4 copy.132
  50.3 5.0 %all-to-all-start.1 = ((f32[128,16,128]{2,1,0:T(8,128)}), f32[128,16,128]{2,1,0:T(8,128)S(1)}, u32[]{:S(2)}, u32[]{:S(2)}) async-start(f32[128,16,128]{2,1,0:T(8,128)} %copy.132), calls=%async_computation.1 | async-start | bytes 2097152 | tf_op jit(solution)/shard_map/all_to_all | solution.py:114
  56.3 12.3 %gather_fusion = bf16[32,128,2,256]{3,2,1,0:T(2,128)(2,1)} fusion(bf16[32,128,2,256]{3,2,1,0:T(2,128)(2,1)} %param.22, s32[1024]{0:T(1024)S(1)} %pad_clamp_fusion.1), kind=kCustom, calls=%fused_computation | custom fusion | bytes 8388736 | tf_op jit(solution)/shard_map/gather | solution.py:144
  68.7 7.4 %all-to-all-done.1 = f32[128,16,128]{2,1,0:T(8,128)S(1)} async-done(((f32[128,16,128]{2,1,0:T(8,128)}), f32[128,16,128]{2,1,0:T(8,128)S(1)}, u32[]{:S(2)}, u32[]{:S(2)}) %all-to-all-start.1) | async-done | bytes 1048608 | tf_op jit(solution)/shard_map/all_to_all | solution.py:114
  76.0 5.0 %all-to-all-start.3 = ((bf16[32,128,2,256]{3,2,1,0:T(2,128)(2,1)}), bf16[32,128,2,256]{3,2,1,0:T(2,128)(2,1)}, u32[]{:S(2)}, u32[]{:S(2)}) async-start(bf16[32,128,2,256]{3,2,1,0:T(2,128)(2,1)} %gather_fusion), calls=%async_computation.3 | async-start | bytes 8388608 | tf_op jit(solution)/shard_map/all_to_all | solution.py:171
  81.4 5.8 %psum.7 = bf16[16,128]{1,0:T(8,128)(2,1)S(1)} all-reduce(f32[16,128]{1,0:T(8,128)S(1)} %fusion.49), channel_id=1, replica_groups=mesh['groups'=2,'seq'=4,'tensor'=4] {'tensor'}, use_global_device_ids=true, to_apply=%region_12.13 | all-reduce | flops 2048 | bytes 12288 | tf_op jit(solution)/shard_map/psum | solution.py:155
  88.9 0.7 reduce.4
  89.7 0.7 reduce.3
  91.1 0.7 copy.168
  91.8 78.9 %all-to-all-done.3 = bf16[32,128,2,256]{3,2,1,0:T(2,128)(2,1)} async-done(((bf16[32,128,2,256]{3,2,1,0:T(2,128)(2,1)}), bf16[32,128,2,256]{3,2,1,0:T(2,128)(2,1)}, u32[]{:S(2)}, u32[]{:S(2)}) %all-to-all-start.3) | async-done | bytes 4194336 | tf_op jit(solution)/shard_map/all_to_all | solution.py:171
  170.8 5.0 %copy.136 = bf16[32,128,2,256]{3,1,2,0:T(8,128)(2,1)} copy(bf16[32,128,2,256]{3,2,1,0:T(2,128)(2,1)} %all-to-all-done.3) | data formatting | bytes 8388608 | tf_op jit(solution)/shard_map/all_to_all | solution.py:171
  175.8 4.9 %gather_fusion.1 = bf16[32,128,2,256]{3,1,2,0:T(8,128)(2,1)} fusion(bf16[32,128,2,256]{3,1,2,0:T(8,128)(2,1)} %copy.136, s32[1024]{0:T(1024)S(1)} %pad_clamp_fusion), kind=kCustom, calls=%fused_computation.1 | custom fusion | bytes 8388736 | tf_op jit(solution)/shard_map/gather | solution.py:172
  180.7 2.5 %copy.137 = bf16[32,128,2,256]{3,1,0,2:T(8,128)(2,1)S(1)} copy(bf16[32,128,2,256]{3,1,2,0:T(8,128)(2,1)} %gather_fusion.1) | data formatting | bytes 8388608 | tf_op jit(solution)/shard_map/gather | solution.py:172
  183.2 2.3 %fusion.45 = (bf16[4,1024,1,256]{3,1,0,2:T(8,128)(2,1)}, bf16[4,1024,1,256]{3,1,0,2:T(8,128)(2,1)}) fusion(bf16[4,1024,2,256]{3,1,0,2:T(8,128)(2,1)S(1)} %bitcast.124), kind=kLoop, calls=%fused_computation.94 | loop fusion | bytes 8388608 | tf_op jit(solution)/shard_map/slice | solution.py:173
  185.5 3.0 %copy.140 = bf16[4,1024,1,256]{1,3,0,2:T(8,128)(2,1)S(1)} copy(bf16[4,1024,1,256]{3,1,0,2:T(8,128)(2,1)} %get-tuple-element.33) | data formatting | bytes 4194304 | tf_op jit(solution)/shard_map/slice | solution.py:173
  188.4 2.6 %copy.141 = bf16[4,1024,2,128]{3,1,2,0:T(8,128)(2,1)} copy(bf16[4,1024,2,128]{1,3,2,0:T(8,128)(2,1)S(1)} %bitcast.125) | data formatting | bytes 4194304 | tf_op jit(solution)/shard_map/concatenate | solution.py:173
  191.0 3.0 %copy.138 = bf16[4,1024,1,256]{1,3,0,2:T(8,128)(2,1)S(1)} copy(bf16[4,1024,1,256]{3,1,0,2:T(8,128)(2,1)} %get-tuple-element.34) | data formatting | bytes 4194304 | tf_op jit(solution)/shard_map/slice | solution.py:174
  194.0 2.6 %copy.139 = bf16[4,1024,2,128]{3,1,2,0:T(8,128)(2,1)} copy(bf16[4,1024,2,128]{1,3,2,0:T(8,128)(2,1)S(1)} %bitcast.126) | data formatting | bytes 4194304 | tf_op jit(solution)/shard_map/concatenate | solution.py:174
  196.6 2.7 %fusion.46 = (f32[4,2,8,4]{2,3,1,0:T(4,128)S(1)}, bf16[4,2,8,4,1028]{4,2,3,1,0:T(8,128)(2,1)S(1)}) fusion(bf16[4,4,2,128]{3,1,2,0:T(4,128)(2,1)S(1)} %bitcast.140, bf16[4,1024,2,128]{3,1,2,0:T(8,128)(2,1)} %copy.141, pred[4,4,1028]{2,1,0:T(4,128)(4,1)S(1)} %pad_add_fusion, bf16[4,4,2,8,128]{4,3,2,1,0:T(8,128)(2,1)S(1)} %reshape.409), kind=kOutput, calls=%fused_computation.95 | convolution fusion | flops 73161728 | bytes 2714688 | tf_op jit(solution)/shard_map/sub | solution.py:37
  200.2 0.7 divide_convert_fusion.1
  (87 shorter events, 6.0 us)
Async XLA Ops:
  0.6 86.8 %copy-start = (bf16[128,2048]{1,0:T(8,128)(2,1)S(1)}, bf16[128,2048]{1,0:T(8,128)(2,1)}, u32[]{:S(2)}) copy-start(bf16[128,2048]{1,0:T(8,128)(2,1)} %param.28) | copy-start | bytes 1572868
  22.7 4.6 %copy-start.1 = (f32[2,1568,128,8]{2,1,3,0:T(8,128)}, f32[2,1568,128,8]{2,1,3,0:T(8,128)S(1)}, u32[]{:S(2)}) copy-start(f32[2,1568,128,8]{2,1,3,0:T(8,128)S(1)} %get-tuple-element.36) | copy-start | bytes 38535172
  22.8 10.8 %copy-start.3 = (bf16[1536,256]{1,0:T(8,128)(2,1)S(1)}, bf16[1536,256]{1,0:T(8,128)(2,1)}, u32[]{:S(2)}) copy-start(bf16[1536,256]{1,0:T(8,128)(2,1)} %param.21) | copy-start | bytes 2359300
  22.8 10.8 %copy-start.7 = (bf16[32,256]{1,0:T(8,128)(2,1)S(1)}, bf16[32,256]{1,0:T(8,128)(2,1)}, u32[]{:S(2)}) copy-start(bf16[32,256]{1,0:T(8,128)(2,1)} %param.19) | copy-start | bytes 49156
  28.1 11.0 %all-to-all-start.2 = ((f32[4,1,512]{2,1,0:T(1,128)}), f32[4,1,512]{2,1,0:T(1,128)S(1)}, u32[]{:S(2)}, u32[]{:S(2)}) async-start(f32[4,1,512]{2,1,0:T(1,128)} %reshape.433), calls=%async_computation.2 | async-start | bytes 16384 | tf_op jit(solution)/shard_map/all_to_all | solution.py:116
  39.1 11.1 %all-to-all-start = ((f32[4,1,512]{2,1,0:T(1,128)}), f32[4,1,512]{2,1,0:T(1,128)S(1)}, u32[]{:S(2)}, u32[]{:S(2)}) async-start(f32[4,1,512]{2,1,0:T(1,128)} %reshape.431), calls=%async_computation | async-start | bytes 16384 | tf_op jit(solution)/shard_map/all_to_all | solution.py:115
  48.8 6.5 %copy-start.11 = (s32[16]{0:T(128)S(1)}, s32[16]{0:T(128)}, u32[]{:S(2)}) copy-start(s32[16]{0:T(128)} %param.29) | copy-start | bytes 196
  48.8 6.5 %copy-start.8 = (s32[16,8]{0,1:T(8,128)S(1)}, s32[16,8]{0,1:T(8,128)}, u32[]{:S(2)}) copy-start(s32[16,8]{0,1:T(8,128)} %param.30) | copy-start | bytes 1540
  50.3 25.8 %all-to-all-start.1 = ((f32[128,16,128]{2,1,0:T(8,128)}), f32[128,16,128]{2,1,0:T(8,128)S(1)}, u32[]{:S(2)}, u32[]{:S(2)}) async-start(f32[128,16,128]{2,1,0:T(8,128)} %copy.132), calls=%async_computation.1 | async-start | bytes 2097152 | tf_op jit(solution)/shard_map/all_to_all | solution.py:114
  68.6 12.5 %copy-start.5 = (bf16[4,4,2048]{2,1,0:T(4,128)(2,1)S(1)}, bf16[4,4,2048]{2,1,0:T(4,128)(2,1)}, u32[]{:S(2)}) copy-start(bf16[4,4,2048]{2,1,0:T(4,128)(2,1)} %param.26) | copy-start | bytes 196612
  68.6 12.5 %copy-start.4 = (bf16[2048,128]{1,0:T(8,128)(2,1)S(1)}, bf16[2048,128]{1,0:T(8,128)(2,1)}, u32[]{:S(2)}) copy-start(bf16[2048,128]{1,0:T(8,128)(2,1)} %param.27) | copy-start | bytes 1572868
  68.6 18.5 %copy-start.9 = (s32[16]{0:T(128)S(1)}, s32[16]{0:T(128)}, u32[]{:S(2)}) copy-start(s32[16]{0:T(128)} %param.32) | copy-start | bytes 196
  68.7 18.5 %copy-start.10 = (s32[16]{0:T(128)S(1)}, s32[16]{0:T(128)}, u32[]{:S(2)}) copy-start(s32[16]{0:T(128)} %param.33) | copy-start | bytes 196
  68.7 19.0 %copy-start.6 = (bf16[4,4,2048]{2,1,0:T(4,128)(2,1)S(1)}, bf16[4,4,2048]{2,1,0:T(4,128)(2,1)}, u32[]{:S(2)}) copy-start(bf16[4,4,2048]{2,1,0:T(4,128)(2,1)} %param.23) | copy-start | bytes 196612
  68.7 19.1 %copy-start.14 = (s32[16]{0:T(128)S(1)}, s32[16]{0:T(128)}, u32[]{:S(2)}) copy-start(s32[16]{0:T(128)} %param.31) | copy-start | bytes 196
  76.0 94.7 %all-to-all-start.3 = ((bf16[32,128,2,256]{3,2,1,0:T(2,128)(2,1)}), bf16[32,128,2,256]{3,2,1,0:T(2,128)(2,1)}, u32[]{:S(2)}, u32[]{:S(2)}) async-start(bf16[32,128,2,256]{3,2,1,0:T(2,128)(2,1)} %gather_fusion), calls=%async_computation.3 | async-start | bytes 8388608 | tf_op jit(solution)/shard_map/all_to_all | solution.py:171
  191.0 5.6 %copy-start.12 = (bf16[4,4,256]{2,1,0:T(4,128)(2,1)S(1)}, bf16[4,4,256]{2,1,0:T(4,128)(2,1)}, u32[]{:S(2)}) copy-start(bf16[4,4,256]{2,1,0:T(4,128)(2,1)} %param.24) | copy-start | bytes 24580
  196.6 2.7 %copy-start.2 = (bf16[4,1024,2,128]{3,1,2,0:T(8,128)(2,1)S(1)}, bf16[4,1024,2,128]{3,1,2,0:T(8,128)(2,1)}, u32[]{:S(2)}) copy-start(bf16[4,1024,2,128]{3,1,2,0:T(8,128)(2,1)} %copy.139) | copy-start | bytes 6291460
  196.6 2.7 %copy-start.13 = (bf16[4,4,256]{2,1,0:T(4,128)(2,1)S(1)}, bf16[4,4,256]{2,1,0:T(4,128)(2,1)}, u32[]{:S(2)}) copy-start(bf16[4,4,256]{2,1,0:T(4,128)(2,1)} %param.25) | copy-start | bytes 24580
where the time goes:
time: 202 us; the launch traced here: 201 us
  waiting for transfers between devices  90.4 us (45%)
  local copies, waits for them, and re-layouts  46.6 us (23%)
  blocking collectives  23.3 us (12%)
  starting transfers between devices  18.7 us (9%)
  matrix products  12.1 us (6%)
  other arithmetic  8.73 us (4%)
    all_to_all x1, waiting for transfers between devices, per_device(): lax.all_to_all(outgoing, 'seq', split_axis=0, concat_axis=0, tiled=True)  78.9 us
    all_gather x1, blocking collectives, per_device(): everyone = lax.all_gather(final_block_queries, 'seq', axis=0, tiled=True)  17.6 us
    gather x1, local copies, waits for them, and re-layouts, per_device(): outgoing = paged_cache_pool[send_place]  12.3 us
    gather x2, local copies, waits for them, and re-layouts, per_device(): incoming[arrive].reshape(slots_here, page_count * page_len, 2, -1)  7.38 us
    all_to_all x1, waiting for transfers between devices, per_device(): lax.all_to_all(summed, 'seq', split_axis=0, concat_axis=0, tiled=True)  7.36 us
    dot_general x2, matrix products, partial_softmax(): jnp.einsum('ekgtp,epkd->etkgd', weights.astype(jnp.bfloat16), value_head_...  6.91 us
    psum x1, blocking collectives, per_device(): lax.psum(jnp.dot(hidden_input_rows, adapter_down_maps, preferred_element_...  5.75 us
    all_to_all x1, starting transfers between devices, per_device(): lax.all_to_all(row_total, 'seq', split_axis=0, concat_axis=0, tiled=True)  5.39 us
  transfers between devices with their start and end apart: 4, of which 3 were waited for; matrix products, arithmetic and copies ran while one was open for 14% of the time, Pallas kernels for 0%

commit v1 on v0

--- a/solution.py
+++ b/solution.py
@@ -6,6 +6,29 @@
 HEAD_SIZE = 128
 LARGEST_RANK = 16
 MASKED = -1e30
+
+
+def in_blocks(value, dim, size):
+    shape = value.shape
+    parts = value.reshape(*shape[:dim], size, shape[dim] // size, *shape[dim + 1 :])
+    return jnp.moveaxis(parts, dim, 0)
+
+
+def laid_out(parts, dim):
+    parts = jnp.moveaxis(parts, 0, dim)
+    lengths = parts.shape
+    return parts.reshape(*lengths[:dim], lengths[dim] * lengths[dim + 1], *lengths[dim + 2 :])
+
+
+def rotated_exchange(x, axis, split_dim, concat_dim):
+    length, index = (lax.axis_size(axis), lax.axis_index(axis))
+    blocks = in_blocks(x, split_dim, length)
+    done = [blocks[index]]
+    for turn in range(1, length):
+        sent = blocks[(index + turn) % length]
+        done.append(lax.ppermute(sent, axis, [(i, (i + turn) % length) for i in range(length)]))
+    blocks = jnp.stack(done)[(index - jnp.arange(length)) % length]
+    return laid_out(blocks, concat_dim)
 
 
 def lookup_rows(lookup, positions):
@@ -168,7 +191,7 @@
     query_vectors = (step_slot_queries.astype(jnp.float32) + raised_queries).astype(jnp.bfloat16)
     step_pos = jnp.arange(decode_step_count, dtype=jnp.int32)
     fresh_ok = step_pos[None, :] <= step_pos[:, None]
-    incoming = lax.all_to_all(outgoing, "seq", split_axis=0, concat_axis=0, tiled=True)
+    incoming = rotated_exchange(outgoing, "seq", 0, 0)
     gathered_pages = incoming[arrive].reshape(slots_here, page_count * page_len, 2, -1)
     all_keys = jnp.concatenate([gathered_pages[:, :, 0], step_token_keys], axis=1)
     all_values = jnp.concatenate([gathered_pages[:, :, 1], step_token_values], axis=1)

time: 202 us -> 216 us (1.069)
  waiting for transfers between devices: 90.4 us -> 2.89 us
  blocking collectives: 23.3 us -> 103 us
  local copies, waits for them, and re-layouts: 46.6 us -> 58.2 us
  other arithmetic: 8.73 us -> 14.7 us
    all_gather x1, blocking collectives: 17.6 us -> 97.2 us  [per_device(): everyone = lax.all_gather(final_block_queries, 'seq', axis=0, tiled=True)]
    all_to_all x1 -> x0, waiting for transfers between devices: 78.9 us -> none  [per_device(): lax.all_to_all(outgoing, 'seq', split_axis=0, concat_axis=0, tiled=True)]
    all_to_all x1, waiting for transfers between devices: 7.36 us -> 0.01 us  [per_device(): lax.all_to_all(summed, 'seq', split_axis=0, concat_axis=0, tiled=True)]
    ppermute x0 -> x3, starting transfers between devices: none -> 6.99 us  [rotated_exchange(): lax.ppermute(sent, axis, [(i, (i + turn) % length) for i in range(length)])]
    all_to_all x1 -> x0, starting transfers between devices: 5.04 us -> none  [per_device(): lax.all_to_all(outgoing, 'seq', split_axis=0, concat_axis=0, tiled=True)]
    all_to_all x1 -> x0, local copies, waits for them, and re-layouts: 5.02 us -> none  [per_device(): lax.all_to_all(outgoing, 'seq', split_axis=0, concat_axis=0, tiled=True)]
    gather x1 -> x2, local copies, waits for them, and re-layouts: 12.3 us -> 17.3 us  [per_device(): outgoing = paged_cache_pool[send_place]]
    gather x0 -> x1, local copies, waits for them, and re-layouts: none -> 4.97 us  [rotated_exchange(): blocks = jnp.stack(done)[(index - jnp.arange(length)) % length]]
  transfers between devices with their start and end apart: 4 -> 6, of which waited for: 3 -> 1; matrix products, arithmetic and copies ran while one was open for 14% -> 27% of each run, Pallas kernels for 0% -> 0%
where the time goes in v1:
time: 216 us; the launch traced here: 215 us
  blocking collectives  103 us (48%)
  local copies, waits for them, and re-layouts  58.2 us (27%)
  starting transfers between devices  20.4 us (9%)
  other arithmetic  14.7 us (7%)
  matrix products  14.1 us (7%)
  waiting for transfers between devices  2.89 us (1%)
    all_gather x1, blocking collectives, per_device(): everyone = lax.all_gather(final_block_queries, 'seq', axis=0, tiled=True)  97.2 us
    gather x2, local copies, waits for them, and re-layouts, per_device(): outgoing = paged_cache_pool[send_place]  17.3 us
    dot_general x2, matrix products, partial_softmax(): jnp.einsum('ekgtp,epkd->etkgd', weights.astype(jnp.bfloat16), value_head_...  8.22 us
    gather x2, local copies, waits for them, and re-layouts, per_device(): incoming[arrive].reshape(slots_here, page_count * page_len, 2, -1)  7.38 us
    ppermute x3, starting transfers between devices, rotated_exchange(): lax.ppermute(sent, axis, [(i, (i + turn) % length) for i in range(length)])  6.99 us
    psum x1, blocking collectives, per_device(): lax.psum(jnp.dot(hidden_input_rows, adapter_down_maps, preferred_element_...  6.02 us
    slice x2, local copies, waits for them, and re-layouts, per_device(): gathered_pages[:, :, 0]  5.2 us
    all_to_all x1, starting transfers between devices, per_device(): lax.all_to_all(row_max, 'seq', split_axis=0, concat_axis=0, tiled=True)  5 us
  transfers between devices with their start and end apart: 6, of which 1 were waited for; matrix products, arithmetic and copies ran while one was open for 27% of the time, Pallas kernels for 0%

profile of v1, /device:TPU:0, one launch (start us, length us, event | category | flops | bytes accessed | tf_op | source)
XLA Modules:
  0.0 214.7 jit_solution(10870751230352460628)
XLA Ops:
  3.1 12.3 %gather_fusion = bf16[32,128,2,256]{3,2,1,0:T(2,128)(2,1)} fusion(bf16[32,128,2,256]{3,2,1,0:T(2,128)(2,1)} %param.22, s32[1024]{0:T(1024)S(1)} %pad_clamp_fusion.2), kind=kCustom, calls=%fused_computation | custom fusion | bytes 8388736 | tf_op jit(solution)/shard_map/gather | solution.py:167
  15.4 5.0 %copy.136 = bf16[32,128,2,256]{3,1,2,0:T(8,128)(2,1)} copy(bf16[32,128,2,256]{3,2,1,0:T(2,128)(2,1)} %gather_fusion) | data formatting | bytes 8388608 | tf_op jit(solution)/shard_map/gather | solution.py:167
  20.4 4.0 %constant_dynamic-slice_fusion.1 = (bf16[1,8,128,2,256]{4,2,3,1,0:T(8,128)(2,1)S(1)}, bf16[8,128,2,256]{3,1,2,0:T(8,128)(2,1)}, bf16[8,128,2,256]{3,1,2,0:T(8,128)(2,1)}, bf16[8,128,2,256]{3,1,2,0:T(8,128)(2,1)}) fusion(bf16[4,8,128,2,256]{4,2,3,1,0:T(8,128)(2,1)} %bitcast.137, s32[]{:T(128)S(6)} %select_n.177, s32[]{:T(128)S(6)} %select_n.183, ...), kind=kLoop, calls=%fused_computation.84 | loop fusion | bytes 8388624 | tf_op jit(solution)/shard_map/dynamic_slice | solution.py:26
  24.4 3.1 %collective-permute-start = (bf16[8,128,2,256]{3,1,2,0:T(8,128)(2,1)}, bf16[8,128,2,256]{3,1,2,0:T(8,128)(2,1)}, u32[]{:S(2)}, u32[]{:S(2)}) collective-permute-start(bf16[8,128,2,256]{3,1,2,0:T(8,128)(2,1)} %get-tuple-element.38), channel_id=1, source_target_pairs={{0,4},{4,8},{8,12},{12,0},{1,5},{5,9},{9,13},{13,1},{2,6},{6,10},{... | collective-permute-start | bytes 3145736 | tf_op jit(solution)/shard_map/ppermute | solution.py:29
  27.5 2.6 %collective-permute-start.1 = (bf16[8,128,2,256]{3,1,2,0:T(8,128)(2,1)}, bf16[8,128,2,256]{3,1,2,0:T(8,128)(2,1)}, u32[]{:S(2)}, u32[]{:S(2)}) collective-permute-start(bf16[8,128,2,256]{3,1,2,0:T(8,128)(2,1)} %get-tuple-element.37), channel_id=1, source_target_pairs={{0,8},{4,12},{8,0},{12,4},{1,9},{5,13},{9,1},{13,5},{2,10},{6,14},... | collective-permute-start | bytes 3145736 | tf_op jit(solution)/shard_map/ppermute | solution.py:29
  30.1 1.3 collective-permute-start.2
  32.7 1.5 copy.124
  34.2 97.2 %all_gather.3 = bf16[128,2048]{1,0:T(8,128)(2,1)} all-gather(bf16[32,2048]{1,0:T(8,128)(2,1)S(1)} %copy-done.7), channel_id=1, replica_groups=mesh['groups'=2,'seq'=4,'tensor'=4] {'seq'}, dimensions={0}, use_global_device_ids=true | all-gather | bytes 655360 | tf_op jit(solution)/shard_map/all_gather | solution.py:114
  131.4 1.3 copy.125
  132.7 2.0 fusion.1
  134.8 3.0 %fusion.2 = f32[2,8,128]{2,1,0:T(8,128)S(1)} fusion(f32[2,1568,128,8]{2,1,3,0:T(8,128)S(1)} %get-tuple-element.40, f32[2,8,128]{2,1,0:T(8,128)S(1)} %get-tuple-element.39, pred[128,1568]{0,1:T(8,128)(4,1)S(1)} %iota_compare_fusion), kind=kLoop, calls=%fused_computation.7 | loop fusion | flops 16054272 | bytes 13062144 | tf_op jit(solution)/shard_map/while/body/eval_jaxpr/reduce_sum | solution.py:61
  137.9 1.7 copy-done.2
  140.3 4.2 %all-to-all-start.2 = ((f32[4,1,512]{2,1,0:T(1,128)}), f32[4,1,512]{2,1,0:T(1,128)S(1)}, u32[]{:S(2)}, u32[]{:S(2)}) async-start(f32[4,1,512]{2,1,0:T(1,128)} %reshape.498), calls=%async_computation.2 | async-start | bytes 16384 | tf_op jit(solution)/shard_map/all_to_all | solution.py:139
  145.0 6.0 %psum.7 = bf16[16,128]{1,0:T(8,128)(2,1)S(1)} all-reduce(f32[16,128]{1,0:T(8,128)S(1)} %fusion.51), channel_id=1, replica_groups=mesh['groups'=2,'seq'=4,'tensor'=4] {'tensor'}, use_global_device_ids=true, to_apply=%region_12.13 | all-reduce | flops 2048 | bytes 12288 | tf_op jit(solution)/shard_map/psum | solution.py:178
  151.5 1.4 copy.130
  152.9 6.7 %fusion.5 = f32[2,128,8,128]{3,1,2,0:T(8,128)S(1)} fusion(bf16[1568,2,128,1]{0,2,3,1:T(8,128)(2,1)} %bitcast.145, f32[2,1568,128,8]{2,1,3,0:T(8,128)} %copy-done.2, f32[2,8,128]{2,1,0:T(8,128)S(1)} %get-tuple-element.39, pred[128,1568]{0,1:T(8,128)(4,1)S(1)} %iota_compare_fusion), kind=kOutput, calls=%fused_computation.10 | convolution fusion | flops 838139904 | bytes 14905344 | tf_op jit(solution)/shard_map/while/body/eval_jaxpr/ekgtp,epkd->etkgd/dot_general | solution.py:62
  161.1 5.0 %all-to-all-start = ((f32[4,1,512]{2,1,0:T(1,128)}), f32[4,1,512]{2,1,0:T(1,128)S(1)}, u32[]{:S(2)}, u32[]{:S(2)}) async-start(f32[4,1,512]{2,1,0:T(1,128)} %reshape.496), calls=%async_computation | async-start | bytes 16384 | tf_op jit(solution)/shard_map/all_to_all | solution.py:138
  166.1 1.4 copy.132
  168.8 2.9 %all-to-all-done = f32[4,1,512]{2,1,0:T(1,128)S(1)} async-done(((f32[4,1,512]{2,1,0:T(1,128)}), f32[4,1,512]{2,1,0:T(1,128)S(1)}, u32[]{:S(2)}, u32[]{:S(2)}) %all-to-all-start) | async-done | bytes 8224 | tf_op jit(solution)/shard_map/all_to_all | solution.py:138
  171.7 4.3 %all-to-all-start.1 = ((f32[128,16,128]{2,1,0:T(8,128)}), f32[128,16,128]{2,1,0:T(8,128)}, u32[]{:S(2)}, u32[]{:S(2)}) async-start(f32[128,16,128]{2,1,0:T(8,128)} %copy.132), calls=%async_computation.1 | async-start | bytes 2097152 | tf_op jit(solution)/shard_map/all_to_all | solution.py:137
  176.9 3.6 %pad_maximum_fusion = bf16[4,8,128,2,256]{4,2,3,1,0:T(8,128)(2,1)} fusion(bf16[1,8,128,2,256]{4,2,3,1,0:T(8,128)(2,1)} %bitcast.23, bf16[1,8,128,2,256]{4,2,3,1,0:T(8,128)(2,1)} %bitcast.21, bf16[1,8,128,2,256]{4,2,3,1,0:T(8,128)(2,1)} %bitcast.19, bf16[1,8,128,2,256]{4,2,3,1,0:T(8,128)(2,1)S(1)} %get-tuple-element.35), kind=kLoop, calls=%fused_computation.12 | loop fusion | flops 6291456 | bytes 8388608 | tf_op jit(solution)/shard_map/stack | solution.py:30
  180.5 5.0 %gather_fusion.1 = bf16[4,8,128,2,256]{4,2,3,1,0:T(8,128)(2,1)} fusion(bf16[4,8,128,2,256]{4,2,3,1,0:T(8,128)(2,1)} %pad_maximum_fusion, s32[1024]{0:T(1024)S(1)} %pad_clamp_fusion.1), kind=kCustom, calls=%fused_computation.1 | custom fusion | bytes 8388624 | tf_op jit(solution)/shard_map/gather | solution.py:30
  185.4 4.9 %gather_fusion.2 = bf16[32,128,2,256]{3,1,2,0:T(8,128)(2,1)} fusion(bf16[32,128,2,256]{3,1,2,0:T(8,128)(2,1)} %bitcast.138, s32[1024]{0:T(1024)S(1)} %pad_clamp_fusion), kind=kCustom, calls=%fused_computation.2 | custom fusion | bytes 8388736 | tf_op jit(solution)/shard_map/gather | solution.py:195
  190.4 2.5 %copy.137 = bf16[32,128,2,256]{3,1,0,2:T(8,128)(2,1)S(1)} copy(bf16[32,128,2,256]{3,1,2,0:T(8,128)(2,1)} %gather_fusion.2) | data formatting | bytes 8388608 | tf_op jit(solution)/shard_map/gather | solution.py:195
  192.8 2.2 %fusion.47 = (bf16[4,1024,1,256]{3,1,0,2:T(8,128)(2,1)}, bf16[4,1024,1,256]{3,1,0,2:T(8,128)(2,1)}) fusion(bf16[4,1024,2,256]{3,1,0,2:T(8,128)(2,1)S(1)} %bitcast.139), kind=kLoop, calls=%fused_computation.107 | loop fusion | bytes 8388608 | tf_op jit(solution)/shard_map/slice | solution.py:196
  195.0 3.0 %copy.140 = bf16[4,1024,1,256]{1,3,0,2:T(8,128)(2,1)S(1)} copy(bf16[4,1024,1,256]{3,1,0,2:T(8,128)(2,1)} %get-tuple-element.33) | data formatting | bytes 4194304 | tf_op jit(solution)/shard_map/slice | solution.py:196
  198.0 2.6 %copy.141 = bf16[4,1024,2,128]{3,1,2,0:T(8,128)(2,1)} copy(bf16[4,1024,2,128]{1,3,2,0:T(8,128)(2,1)S(1)} %bitcast.140) | data formatting | bytes 4194304 | tf_op jit(solution)/shard_map/concatenate | solution.py:196
  200.6 3.0 %copy.138 = bf16[4,1024,1,256]{1,3,0,2:T(8,128)(2,1)S(1)} copy(bf16[4,1024,1,256]{3,1,0,2:T(8,128)(2,1)} %get-tuple-element.34) | data formatting | bytes 4194304 | tf_op jit(solution)/shard_map/slice | solution.py:197
  203.6 2.6 %copy.139 = bf16[4,1024,2,128]{3,1,2,0:T(8,128)(2,1)} copy(bf16[4,1024,2,128]{1,3,2,0:T(8,128)(2,1)S(1)} %bitcast.141) | data formatting | bytes 4194304 | tf_op jit(solution)/shard_map/concatenate | solution.py:197
  206.2 3.5 %fusion.48 = (f32[4,2,8,4]{2,3,1,0:T(4,128)S(1)}, bf16[4,2,8,4,1028]{4,2,3,1,0:T(8,128)(2,1)}) fusion(bf16[4,4,2,128]{3,1,2,0:T(4,128)(2,1)S(1)} %bitcast.154, bf16[4,1024,2,128]{3,1,2,0:T(8,128)(2,1)} %copy.141, pred[4,4,1028]{2,1,0:T(4,128)(4,1)S(1)} %pad_add_fusion, bf16[4,4,2,8,128]{4,3,2,1,0:T(8,128)(2,1)S(1)} %reshape.466), kind=kOutput, calls=%fused_computation.108 | convolution fusion | flops 73161728 | bytes 2714688 | tf_op jit(solution)/shard_map/sub | solution.py:60
  209.7 1.5 fusion.18
  212.3 1.6 multiply_reduce_fusion
  (102 shorter events, 10.8 us)
Async XLA Ops:
  0.6 159.3 %copy-start = (bf16[128,2048]{1,0:T(8,128)(2,1)S(1)}, bf16[128,2048]{1,0:T(8,128)(2,1)}, u32[]{:S(2)}) copy-start(bf16[128,2048]{1,0:T(8,128)(2,1)} %param.28) | copy-start | bytes 1572868
  20.4 11.3 %copy-start.4 = (bf16[1536,256]{1,0:T(8,128)(2,1)S(1)}, bf16[1536,256]{1,0:T(8,128)(2,1)}, u32[]{:S(2)}) copy-start(bf16[1536,256]{1,0:T(8,128)(2,1)} %param.20) | copy-start | bytes 2359300
  20.4 11.3 %copy-start.10 = (bf16[32,256]{1,0:T(8,128)(2,1)S(1)}, bf16[32,256]{1,0:T(8,128)(2,1)}, u32[]{:S(2)}) copy-start(bf16[32,256]{1,0:T(8,128)(2,1)} %param.18) | copy-start | bytes 49156
  20.4 13.8 %copy-start.7 = (bf16[32,2048]{1,0:T(8,128)(2,1)S(1)}, bf16[32,2048]{1,0:T(8,128)(2,1)}, u32[]{:S(2)}) copy-start(bf16[32,2048]{1,0:T(8,128)(2,1)} %param.17) | copy-start | bytes 393220
  24.4 152.4 %collective-permute-start = (bf16[8,128,2,256]{3,1,2,0:T(8,128)(2,1)}, bf16[8,128,2,256]{3,1,2,0:T(8,128)(2,1)}, u32[]{:S(2)}, u32[]{:S(2)}) collective-permute-start(bf16[8,128,2,256]{3,1,2,0:T(8,128)(2,1)} %get-tuple-element.38), channel_id=1, source_target_pairs={{0,4},{4,8},{8,12},{12,0},{1,5},{5,9},{9,13},{13,1},{2,6},{6,10},{... | collective-permute-start | bytes 3145736 | tf_op jit(solution)/shard_map/ppermute | solution.py:29
  27.5 149.4 %collective-permute-start.1 = (bf16[8,128,2,256]{3,1,2,0:T(8,128)(2,1)}, bf16[8,128,2,256]{3,1,2,0:T(8,128)(2,1)}, u32[]{:S(2)}, u32[]{:S(2)}) collective-permute-start(bf16[8,128,2,256]{3,1,2,0:T(8,128)(2,1)} %get-tuple-element.37), channel_id=1, source_target_pairs={{0,8},{4,12},{8,0},{12,4},{1,9},{5,13},{9,1},{13,5},{2,10},{6,14},... | collective-permute-start | bytes 3145736 | tf_op jit(solution)/shard_map/ppermute | solution.py:29
  30.1 146.8 %collective-permute-start.2 = (bf16[8,128,2,256]{3,1,2,0:T(8,128)(2,1)}, bf16[8,128,2,256]{3,1,2,0:T(8,128)(2,1)}, u32[]{:S(2)}, u32[]{:S(2)}) collective-permute-start(bf16[8,128,2,256]{3,1,2,0:T(8,128)(2,1)} %get-tuple-element.36), channel_id=1, source_target_pairs={{0,12},{4,0},{8,4},{12,8},{1,13},{5,1},{9,5},{13,9},{2,14},{6,2},{... | collective-permute-start | bytes 3145736 | tf_op jit(solution)/shard_map/ppermute | solution.py:29
  134.8 4.8 %copy-start.2 = (f32[2,1568,128,8]{2,1,3,0:T(8,128)}, f32[2,1568,128,8]{2,1,3,0:T(8,128)S(1)}, u32[]{:S(2)}) copy-start(f32[2,1568,128,8]{2,1,3,0:T(8,128)S(1)} %get-tuple-element.40) | copy-start | bytes 38535172
  134.8 10.0 %copy-start.12 = (s32[16]{0:T(128)S(1)}, s32[16]{0:T(128)}, u32[]{:S(2)}) copy-start(s32[16]{0:T(128)} %param.29) | copy-start | bytes 196
  134.8 10.1 %copy-start.8 = (bf16[4,4,2048]{2,1,0:T(4,128)(2,1)S(1)}, bf16[4,4,2048]{2,1,0:T(4,128)(2,1)}, u32[]{:S(2)}) copy-start(bf16[4,4,2048]{2,1,0:T(4,128)(2,1)} %param.26) | copy-start | bytes 196612
  134.8 10.1 %copy-start.6 = (bf16[2048,128]{1,0:T(8,128)(2,1)S(1)}, bf16[2048,128]{1,0:T(8,128)(2,1)}, u32[]{:S(2)}) copy-start(bf16[2048,128]{1,0:T(8,128)(2,1)} %param.27) | copy-start | bytes 1572868
  134.8 16.3 %copy-start.17 = (s32[16]{0:T(128)S(1)}, s32[16]{0:T(128)}, u32[]{:S(2)}) copy-start(s32[16]{0:T(128)} %param.31) | copy-start | bytes 196
  134.8 16.6 %copy-start.5 = (bf16[1536,256]{1,0:T(8,128)(2,1)S(1)}, bf16[1536,256]{1,0:T(8,128)(2,1)}, u32[]{:S(2)}) copy-start(bf16[1536,256]{1,0:T(8,128)(2,1)} %param.21) | copy-start | bytes 2359300
  134.8 16.6 %copy-start.11 = (bf16[32,256]{1,0:T(8,128)(2,1)S(1)}, bf16[32,256]{1,0:T(8,128)(2,1)}, u32[]{:S(2)}) copy-start(bf16[32,256]{1,0:T(8,128)(2,1)} %param.19) | copy-start | bytes 49156
  140.3 20.7 %all-to-all-start.2 = ((f32[4,1,512]{2,1,0:T(1,128)}), f32[4,1,512]{2,1,0:T(1,128)S(1)}, u32[]{:S(2)}, u32[]{:S(2)}) async-start(f32[4,1,512]{2,1,0:T(1,128)} %reshape.498), calls=%async_computation.2 | async-start | bytes 16384 | tf_op jit(solution)/shard_map/all_to_all | solution.py:139
  152.9 6.8 %copy-start.13 = (s32[16]{0:T(128)S(1)}, s32[16]{0:T(128)}, u32[]{:S(2)}) copy-start(s32[16]{0:T(128)} %param.32) | copy-start | bytes 196
  152.9 6.8 %copy-start.14 = (s32[16]{0:T(128)S(1)}, s32[16]{0:T(128)}, u32[]{:S(2)}) copy-start(s32[16]{0:T(128)} %param.33) | copy-start | bytes 196
  152.9 7.3 %copy-start.9 = (bf16[4,4,2048]{2,1,0:T(4,128)(2,1)S(1)}, bf16[4,4,2048]{2,1,0:T(4,128)(2,1)}, u32[]{:S(2)}) copy-start(bf16[4,4,2048]{2,1,0:T(4,128)(2,1)} %param.23) | copy-start | bytes 196612
  161.1 10.6 %all-to-all-start = ((f32[4,1,512]{2,1,0:T(1,128)}), f32[4,1,512]{2,1,0:T(1,128)S(1)}, u32[]{:S(2)}, u32[]{:S(2)}) async-start(f32[4,1,512]{2,1,0:T(1,128)} %reshape.496), calls=%async_computation | async-start | bytes 16384 | tf_op jit(solution)/shard_map/all_to_all | solution.py:138
  171.7 40.6 %all-to-all-start.1 = ((f32[128,16,128]{2,1,0:T(8,128)}), f32[128,16,128]{2,1,0:T(8,128)}, u32[]{:S(2)}, u32[]{:S(2)}) async-start(f32[128,16,128]{2,1,0:T(8,128)} %copy.132), calls=%async_computation.1 | async-start | bytes 2097152 | tf_op jit(solution)/shard_map/all_to_all | solution.py:137
  200.6 5.6 %copy-start.15 = (bf16[4,4,256]{2,1,0:T(4,128)(2,1)S(1)}, bf16[4,4,256]{2,1,0:T(4,128)(2,1)}, u32[]{:S(2)}) copy-start(bf16[4,4,256]{2,1,0:T(4,128)(2,1)} %param.24) | copy-start | bytes 24580
  206.2 3.5 %copy-start.3 = (bf16[4,1024,2,128]{3,1,2,0:T(8,128)(2,1)S(1)}, bf16[4,1024,2,128]{3,1,2,0:T(8,128)(2,1)}, u32[]{:S(2)}) copy-start(bf16[4,1024,2,128]{3,1,2,0:T(8,128)(2,1)} %copy.139) | copy-start | bytes 6291460
  206.2 3.5 %copy-start.16 = (bf16[4,4,256]{2,1,0:T(4,128)(2,1)S(1)}, bf16[4,4,256]{2,1,0:T(4,128)(2,1)}, u32[]{:S(2)}) copy-start(bf16[4,4,256]{2,1,0:T(4,128)(2,1)} %param.25) | copy-start | bytes 24580
  206.2 8.5 %copy-start.1 = (bf16[128,2048]{1,0:T(8,128)(2,1)S(1)}, bf16[128,2048]{1,0:T(8,128)(2,1)}, u32[]{:S(2)}) copy-start(bf16[128,2048]{1,0:T(8,128)(2,1)} %param.28) | copy-start | bytes 1572868
